TPU v7x, 32 devices: a whole 2x2x4 slice. The times are simulated.
32 devices in a mesh: vox: 16 (over z, x, core), subj: 2 (over y).
Axes of the slice: x: 2, y: 2, z: 4, core: 2. Of those that a mesh axis runs over, the one named last changes fastest.
Arguments:
- series: bfloat16 [8, 4096, 512], P('subj', 'vox'), may hold values from -6 to 6
- live_mask: int32 [4096], P('vox'), may hold values from 0 to 1, as said below
- neighbours: int32 [4096, 13], P('vox'), may hold values from -1 to 510, as said below
- start_vectors: float32 [4096, 64], P('vox'), may hold values from -60 to 60
Outputs:
- embedding: float32 [4096, 64], P('vox')
Inputs may be any that keep to these rules, and one draw needn't show every extreme that they name: `live_mask`: within each aligned block of 128 voxel slots the live slots are a leading run of 1 to 128 slots. `neighbours`: slot n of voxel i names voxel (i // 256 - 1) * 256 + n, which is live and lies before i; the entries of a row are distinct or -1; rows of dead voxels are all -1; rows of the first 256 voxels name no slot under 256.
All inputs are finite; a program needn't handle non-finite values.
Results may differ from a plain program's by a relative error of at most 0.0024.
Values may be sent and summed in bfloat16 or wider, within the bound.
No kernel may reach another device: no remote copies, remote signals or barrier semaphores. Data moves between devices by JAX's collectives and lax.ppermute only.
A program may use at most 64 MiB of HBM per device.

v0:
```python
import functools
import math

import jax
import jax.numpy as jnp
from jax import lax
from jax.experimental import pallas as pl
from jax.experimental.pallas import tpu as pltpu
from jax.sharding import PartitionSpec as P


ITERS = 3
UNIT = 4
WELL_CONDITIONED = 64.0


NT = (((1,), (1,)), ((), ()))
NN = (((1,), (0,)), ((), ()))
VMEM = pl.BlockSpec(memory_space=pltpu.VMEM)


def dot(left, right, dims=NN, precision=None):
    return lax.dot_general(
        left, right, dims, precision=precision, preferred_element_type=jnp.float32
    )


def exchanged(value, axis, distance):
    count = lax.axis_size(axis)
    return lax.ppermute(value, axis, [(i, i ^ distance) for i in range(count)])


def summed_over(value, axis, stride=1):
    count = lax.axis_size(axis)
    if count & (count - 1):
        return lax.psum(value, axis) / stride
    while stride < count:
        if stride > 1 and 4 * stride <= count:
            first, second, third = (exchanged(value, axis, k * stride) for k in (1, 2, 3))
            value = (value + first) + (second + third)
            stride *= 4
        else:
            value = value + exchanged(value, axis, stride)
            stride *= 2
    return value


def shifted(shard, axis, by):
    count = lax.axis_size(axis)
    pairs = [(i, i + by) for i in range(count) if 0 <= i + by < count]
    return lax.ppermute(shard, axis, pairs)


def standardize(z_ref, s, series_ref, q):
    width = series_ref.shape[1]
    for start in range(0, width, 32):
        values = series_ref[q, start : start + 32, :].astype(jnp.float32)
        center = values - jnp.mean(values, axis=-1, keepdims=True)
        spread = jnp.mean(center * center, axis=-1, keepdims=True)
        z_ref[s, start : start + 32, :] = (center * lax.rsqrt(spread + 1e-05)).astype(jnp.bfloat16)


def picked_sums(corr_ref, marks_ref, first_mark, offsets):
    slots, width = corr_ref.shape
    marks = [jnp.broadcast_to(marks_ref[k : k + 1, :], (8, width)) for k in range(offsets)]
    row = lax.broadcasted_iota(jnp.int32, (8, width), 0) + first_mark
    sums = [jnp.zeros((8, width), jnp.float32) for _ in range(offsets)]
    for start in range(0, slots, 8):
        values = corr_ref[start : start + 8, :]
        for k in range(offsets):
            sums[k] = sums[k] + jnp.where(marks[k] == row + start, values, 0.0)
    return [jnp.sum(s, axis=0, keepdims=True) for s in sums]


def own_kernel(offsets, series_ref, marks_ref, z_ref, sums_ref, corr_ref):
    subjects, width, _ = series_ref.shape
    total = None
    for s in range(subjects):
        standardize(z_ref, s, series_ref, s)
        part = dot(z_ref[s], z_ref[s], NT)
        total = part if total is None else total + part
    corr_ref[...] = total
    sums_ref[...] = jnp.zeros_like(sums_ref)
    for k, row in enumerate(picked_sums(corr_ref, marks_ref, width + 1, offsets)):
        sums_ref[k : k + 1, :] = row


def earlier_kernel(offsets, series_ref, z_ref, marks_ref, own_ref, sums_ref, zs_ref, corr_ref):
    subjects = series_ref.shape[0]
    total = None
    for s in range(subjects):
        standardize(zs_ref, s, series_ref, s)
        part = dot(zs_ref[s], z_ref[s], NT)
        total = part if total is None else total + part
    corr_ref[...] = total
    sums_ref[...] = own_ref[...]
    for k, row in enumerate(picked_sums(corr_ref, marks_ref, 1, offsets)):
        sums_ref[k : k + 1, :] += row


def chosen(flag, yes, no):
    return jnp.where(flag, yes, no)


def in_order(flags_ref, own, three, four):
    odd = flags_ref[1] == 1
    return chosen(odd, three, four), own, chosen(odd, four, three)


def own_data_kernel(vectors_ref, neighbours_ref, live_ref, data_ref, marks_ref):
    vecs = vectors_ref.shape[0]
    offsets, _ = neighbours_ref.shape
    living = live_ref[...].astype(jnp.float32)
    marks = neighbours_ref[...] + 1
    marks_ref[...] = marks
    data_ref[...] = jnp.zeros_like(data_ref)
    data_ref[:vecs, :] = vectors_ref[...] * living
    data_ref[vecs : vecs + offsets, :] = marks.astype(jnp.float32)
    data_ref[vecs + offsets : vecs + offsets + 1, :] = living


def compact_kernel(vecs, data_ref, partner_ref, row_ref):
    for j, ref in enumerate((data_ref, partner_ref)):
        marks = ref[vecs:, :].astype(jnp.int32)
        digits = jnp.concatenate([marks // 16, marks % 16], axis=0)
        row_ref[j, :vecs, :] = ref[:vecs, :].astype(jnp.bfloat16)
        row_ref[j, vecs:, :] = digits.astype(jnp.float32).astype(jnp.bfloat16)


def stack_kernel(vecs, flags_ref, data_ref, partner_ref, three_ref, four_ref, stack_ref):
    nrows = data_ref.shape[0] - vecs
    for j, ref in enumerate((data_ref, partner_ref)):
        parts = in_order(flags_ref, ref[...], three_ref[j], four_ref[j])
        for w, part in enumerate(parts):
            part = part.astype(jnp.float32)
            stack_ref[2 * w + j, :vecs, :] = part[:vecs]
            marks = part[vecs:]
            if w != 1:
                marks = 16.0 * marks[:nrows] + marks[nrows:]
            stack_ref[2 * w + j, vecs:, :] = marks


def find_entries(offsets, vecs, place, data_ref, which_ref, marks_ref):
    width = data_ref.shape[2]
    nrows = marks_ref.shape[1]
    for i in range(data_ref.shape[0]):
        marks_ref[i] = data_ref[i, vecs:, :].astype(jnp.int32)
    chunk = 128
    pieces = width // chunk
    base = lax.broadcasted_iota(jnp.int32, (chunk, width), 0) + (width + 1)

    def dense(step, carry):
        i = step // pieces
        start = pl.multiple_of((step % pieces) * chunk, chunk)
        rows = base + start
        value = jnp.full((chunk, width), nrows - 1, jnp.int32)
        for k in range(offsets):
            value = jnp.where(marks_ref[i, k : k + 1, :] == rows, k, value)
        b = UNIT * (i // 2) + lax.bitwise_xor(place, 2 * (i % 2))
        which_ref[b, pl.ds(start, chunk), :] = value
        return carry

    lax.fori_loop(0, data_ref.shape[0] * pieces, dense, 0)


def same_window_kernel(offsets, vecs, flags_ref, same_ref, which_ref, marks_ref):
    find_entries(offsets, vecs, flags_ref[0], same_ref, which_ref, marks_ref)


def other_window_kernel(
    offsets, vecs, flags_ref, same_ref, other_ref, _, which_ref, vec_ref, row_ref, marks_ref
):
    place = flags_ref[0]
    for i in range(same_ref.shape[0]):
        for ref, lift in ((same_ref, 0), (other_ref, 1)):
            b = UNIT * (i // 2) + lax.bitwise_xor(place, 2 * (i % 2) + lift)
            vec_ref[b] = ref[i, :vecs, :]
            row_ref[b] = ref[i, vecs:, :]
    find_entries(offsets, vecs, lax.bitwise_xor(place, 1), other_ref, which_ref, marks_ref)


def graph_kernel(offsets, flags_ref, *refs):
    row_ref, three_ref, four_ref = refs[:3]
    which_ref, vec_ref, data_ref = refs[3:6]
    y_ref, gram_ref = refs[6:8]
    graph_ref, weight_ref, mark_ref, scale_ref = refs[8:]
    vecs, width = y_ref.shape
    count, nrows = weight_ref.shape[:2]
    place = flags_ref[0]
    for r in range(UNIT):
        weights = in_order(flags_ref, row_ref[r], three_ref[r], four_ref[r])
        for w in range(3):
            b = UNIT * w + lax.bitwise_xor(place, r)
            weight_ref[b] = weights[w].astype(jnp.float32)
            mark_ref[b] = data_ref[b].astype(jnp.int32)

    chunk = 64
    base = lax.broadcasted_iota(jnp.int32, (chunk, width), 0) + 1

    def dense(b, carry):
        for lane in range(0, width, 128):
            tables = [weight_ref[b, g : g + 8, lane : lane + 128] for g in range(0, nrows, 8)]
            for row in range(0, width, 16):
                halves = []
                for start in (row, row + 8):
                    which = which_ref[b, start : start + 8, lane : lane + 128]
                    low = jnp.bitwise_and(which, 7)
                    value = None
                    for g, table in enumerate(tables):
                        entry = jnp.take_along_axis(table, low, axis=0, mode="promise_in_bounds")
                        value = entry if g == 0 else jnp.where(which >= 8 * g, entry, value)
                    halves.append(value)
                graph_ref[b, width + row : width + row + 16, lane : lane + 128] = jnp.concatenate(
                    halves, axis=0
                ).astype(jnp.bfloat16)
        for start in range(0, width, chunk):
            value = jnp.zeros((chunk, width), jnp.float32)
            for k in range(offsets):
                value = jnp.where(
                    mark_ref[b + 1, k : k + 1, :] == base + start,
                    weight_ref[b + 1, k : k + 1, :],
                    value,
                )
            graph_ref[b + 1, start : start + chunk, :] = value.astype(jnp.bfloat16)
        inside = graph_ref[b, width : 2 * width, :]
        inside_t, after = inside.T, graph_ref[b + 1, :width, :].T
        graph_ref[b, width : 2 * width, :] = inside + inside_t
        graph_ref[b, 2 * width :, :] = after
        owed = jnp.sum(inside_t.astype(jnp.float32) + after.astype(jnp.float32), axis=0)
        degree = 1.0 + jnp.sum(weight_ref[b], axis=0, keepdims=True) + owed[None, :]
        live = data_ref[b, offsets : offsets + 1, :]
        scale_ref[b] = jnp.broadcast_to(live * lax.rsqrt(degree), scale_ref.shape[1:])
        return carry

    lax.fori_loop(1, count - 1, dense, 0)

    scales = {b: scale_ref[b, 0:1, :] for b in range(1, count - 1)}
    vectors = {b: vec_ref[b] for b in range(1, count - 1)}
    for step in range(ITERS):
        scaled, sent = {}, {}
        for b in vectors:
            scaled[b] = scales[b] * vectors[b]
            high = scaled[b].astype(jnp.bfloat16)
            low = (scaled[b] - high.astype(jnp.float32)).astype(jnp.bfloat16)
            sent[b] = jnp.concatenate([high, low], axis=0)
        images = {}
        for b in range(step + 2, count - 2 - step):
            window = jnp.concatenate([sent[b - 1], sent[b], sent[b + 1]], axis=1)
            both = dot(window, graph_ref[b])
            edges = both[:vecs] + both[vecs:]
            images[b] = 0.5 * (vectors[b] + scales[b] * (scaled[b] + edges))
        vectors = images
    ours = [vectors[UNIT + r] for r in range(UNIT)]
    y = ours[0]
    for r in range(1, UNIT):
        y = chosen(place == r, ours[r], y)
    y_ref[...] = y
    joined = jnp.concatenate(ours, axis=1)
    gram = dot(joined, joined, NT, lax.Precision.HIGHEST)
    half = vecs // 2
    gram_ref[...] = jnp.concatenate([gram[:half], gram[half:]], axis=1)


def factor_kernel(gram_ref, inverse_ref, bound_ref, work_ref):
    vecs = inverse_ref.shape[0]
    packed = gram_ref[...]
    gram = jnp.concatenate([packed[:, :vecs], packed[:, vecs:]], axis=0)
    row = lax.broadcasted_iota(jnp.int32, (vecs, vecs), 0)
    lane = lax.broadcasted_iota(jnp.int32, (vecs, vecs), 1)
    eye = (row == lane).astype(jnp.float32)
    full = jnp.concatenate([gram, eye], axis=1)
    blocks = [full[i : i + 8, :] for i in range(0, vecs, 8)]
    count = len(blocks)
    wide = 2 * vecs
    sub = lax.broadcasted_iota(jnp.int32, (8, wide), 0)
    for p in range(count):
        columns = [
            [jnp.broadcast_to(b[:, 8 * p + t : 8 * p + t + 1], (8, wide)) for b in blocks[p:]]
            for t in range(8)
        ]
        for t in range(8):
            pivot = jnp.broadcast_to(columns[t][0][t : t + 1, :], (8, wide))
            inverse = 1.0 / pivot
            line = jnp.broadcast_to(blocks[p][t : t + 1, :], (8, wide))
            j = 8 * p + t
            work_ref[j : j + 1, :] = (line * lax.rsqrt(pivot))[0:1, :]
            if j == vecs - 1:
                break
            times = [c * inverse for c in columns[t]]
            times[0] = jnp.where(sub > t, times[0], 0.0)
            later = [
                jnp.broadcast_to(columns[u][0][t : t + 1, :], (8, wide)) for u in range(t + 1, 8)
            ]
            for i in range(p, count):
                m = times[i - p]
                blocks[i] = blocks[i] - m * line
                for u in range(t + 1, 8):
                    columns[u][i - p] = columns[u][i - p] - m * later[u - t - 1]
    inverse_factor = work_ref[:, vecs:]
    diagonal = jnp.sum(gram * eye, axis=0, keepdims=True)
    bound_ref[0, 0] = jnp.sum(inverse_factor * inverse_factor * diagonal)
    inverse_ref[...] = inverse_factor


def solve_kernel(inverse_ref, y_ref, x_ref):
    x_ref[...] = dot(inverse_ref[...], y_ref[...], NN, lax.Precision.HIGHEST)


def dense_graph(weight, slots, columns_total):
    column_ids = jnp.arange(columns_total, dtype=jnp.int32)
    matrix = jnp.zeros((weight.shape[0], columns_total), jnp.float32)
    for offset in range(weight.shape[1]):
        hits = (slots[:, offset][:, None] == column_ids[None, :]).astype(jnp.float32)
        matrix = matrix + weight[:, offset][:, None] * hits
    return matrix


def product(left, right):
    return jnp.dot(left, right, precision=lax.Precision.HIGHEST)


def step_by_step(summed, scale, live_mask, neighbours, start_vectors):
    voxels_here = start_vectors.shape[0]
    weight = jnp.where(neighbours >= 0, jnp.exp(scale * summed), 0.0)
    living = live_mask.astype(jnp.float32)
    local_graph = dense_graph(weight, neighbours, 2 * voxels_here)
    owed = jnp.sum(local_graph, axis=0)
    received = shifted(owed[:voxels_here], "vox", -1)
    degree = 1.0 + jnp.sum(weight, axis=1) + owed[voxels_here:] + received
    scaling = living * lax.rsqrt(degree)
    vectors = living[:, None] * start_vectors

    def once(_, vectors):
        scaled = scaling[:, None] * vectors
        earlier_rows = shifted(scaled, "vox", 1)
        window_rows = jnp.concatenate([earlier_rows, scaled], axis=0)
        forward = product(local_graph, window_rows)
        returns = product(local_graph.T, scaled)
        arrived = shifted(returns[:voxels_here], "vox", -1)
        images = 0.5 * (
            vectors + scaling[:, None] * (scaled + forward + returns[voxels_here:] + arrived)
        )
        gram_matrix = summed_over(product(images.T, images), "vox")
        factor = jnp.linalg.cholesky(gram_matrix)
        return lax.linalg.triangular_solve(
            factor, images, left_side=False, lower=True, transpose_a=True
        )

    return lax.fori_loop(0, ITERS, once, vectors)


def call(kernel, outs, *args, scratch=(), out_specs=None, first=VMEM, vmem=16, aliases=None):
    return pl.pallas_call(
        kernel,
        out_shape=outs,
        in_specs=[first] + [VMEM] * (len(args) - 1),
        out_specs=out_specs or jax.tree.map(lambda _: VMEM, outs),
        scratch_shapes=list(scratch),
        cost_estimate=pl.CostEstimate(flops=1_000_000, bytes_accessed=1 << 18, transcendentals=0),
        input_output_aliases=aliases or {},
        compiler_params=pltpu.CompilerParams(vmem_limit_bytes=vmem << 20),
    )(*args)


def pairwise(value, distance, late):
    count = lax.axis_size("vox")
    pairs = [(i, ((i + late) ^ distance) - late) for i in range(count)]
    return lax.ppermute(value, "vox", [(i, j) for i, j in pairs if 0 <= j < count])


def on_device(series, live_mask, neighbours, start_vectors):
    subjects, width, frames = series.shape
    offsets = neighbours.shape[1]
    vecs = start_vectors.shape[1]
    shape = jax.ShapeDtypeStruct
    f32 = jnp.float32
    groups = lax.axis_size("subj")
    scale = 0.5 / math.sqrt(frames * subjects * groups)
    rows = -(-(offsets + 1) // 8) * 8
    smem = pl.BlockSpec(memory_space=pltpu.SMEM)
    number = lax.axis_index("vox").astype(jnp.int32)
    flags = jnp.stack([number % UNIT, (number // UNIT) % 2])
    square = pltpu.VMEM((width, width), f32)

    arriving = shifted(series, "vox", 1)

    data, marks = call(
        own_data_kernel,
        (shape((vecs + rows, width), f32), shape((offsets, width), jnp.int32)),
        start_vectors.T,
        neighbours.T,
        live_mask[None, :],
    )
    data_partner = exchanged(data, "vox", 2)
    data_row = call(
        functools.partial(compact_kernel, vecs),
        shape((2, vecs + 2 * rows, width), jnp.bfloat16),
        data,
        data_partner,
    )
    data_rows = [pairwise(data_row, UNIT, late) for late in (0, UNIT)]
    data_same = call(
        functools.partial(stack_kernel, vecs),
        shape((6, vecs + rows, width), f32),
        flags,
        data,
        data_partner,
        *data_rows,
        first=smem,
    )
    data_other = exchanged(data_same, "vox", 1)
    blocks = 3 * UNIT
    entries = shape((blocks, width, width), jnp.int32)
    marks_scratch = pltpu.VMEM((6, rows, width), jnp.int32)
    half_which = call(
        functools.partial(same_window_kernel, offsets, vecs),
        entries,
        flags,
        data_same,
        first=smem,
        scratch=[marks_scratch],
    )
    window = call(
        functools.partial(other_window_kernel, offsets, vecs),
        (entries, shape((blocks, vecs, width), f32), shape((blocks, rows, width), f32)),
        flags,
        data_same,
        data_other,
        half_which,
        first=smem,
        scratch=[marks_scratch],
        aliases={3: 0},
    )
    z, own = call(
        functools.partial(own_kernel, offsets),
        (shape(series.shape, jnp.bfloat16), shape((rows, width), f32)),
        series,
        marks,
        scratch=[square],
    )
    partial_sums = call(
        functools.partial(earlier_kernel, offsets),
        shape((rows, width), f32),
        arriving,
        z,
        marks,
        own,
        scratch=[pltpu.VMEM(series.shape, jnp.bfloat16), square],
    )

    summed = summed_over(partial_sums, "subj")
    listed = lax.broadcasted_iota(jnp.int32, summed.shape, 0) < offsets
    present = jnp.logical_and(listed, data[vecs:, :] > 0.5)
    weight = jnp.where(present, jnp.exp(scale * summed), 0.0).astype(jnp.bfloat16)
    near = [weight]
    for r in range(1, UNIT):
        near.append(exchanged(weight, "vox", r))
    row = jnp.stack(near)
    rows_around = [pairwise(row, UNIT, late) for late in (0, UNIT)]

    y, gram = call(
        functools.partial(graph_kernel, offsets),
        (shape((vecs, width), f32), shape((vecs // 2, 2 * vecs), f32)),
        flags,
        row,
        *rows_around,
        *window,
        scratch=[
            pltpu.VMEM((blocks, 3 * width, width), jnp.bfloat16),
            pltpu.VMEM((blocks, rows, width), f32),
            pltpu.VMEM((blocks, rows, width), jnp.int32),
            pltpu.VMEM((blocks, 8, width), f32),
        ],
        first=smem,
        vmem=24,
    )
    gram = summed_over(gram, "vox", UNIT)
    inverse_factor, bound = call(
        factor_kernel,
        (shape((vecs, vecs), f32), shape((1, 1), f32)),
        gram,
        out_specs=(VMEM, smem),
        scratch=[pltpu.VMEM((vecs, 2 * vecs), f32)],
    )
    return lax.cond(
        bound[0, 0] <= WELL_CONDITIONED * vecs,
        lambda: call(solve_kernel, shape((vecs, width), f32), inverse_factor, y).T,
        lambda: step_by_step(
            summed[:offsets].T, scale, live_mask, neighbours, start_vectors
        ),
    )


def solution(mesh):
    placed = (P("subj", "vox", None), P("vox"), P("vox", None), P("vox", None))
    return jax.shard_map(
        on_device, mesh=mesh, in_specs=placed, out_specs=P("vox", None), check_vma=False
    )
```

profile of v0, /device:TPU:0, one launch (start us, length us, event | category | flops | bytes accessed | tf_op | source)
XLA Modules:
  0.0 64.7 jit_solution(17656284446469739345)
XLA Ops:
  0.0 2.5 %collective-permute-start.8 = (bf16[4,256,512]{2,1,0:T(8,128)(2,1)}, bf16[4,256,512]{2,1,0:T(8,128)(2,1)S(1)}, u32[]{:S(2)}, u32[]{:S(2)}) collective-permute-start(bf16[4,256,512]{2,1,0:T(8,128)(2,1)} %series_ref.1), channel_id=1, source_target_pairs={{0,2},{2,4},{4,6},{6,8},{8,10},{10,12},{12,14},{14,16},{16,18},{18... | collective-permute-start | bytes 3145736 | tf_op jit(solution)/shard_map/ppermute | solution.py:51
  2.5 0.9 %shard_map.48 = (f32[80,256]{1,0:T(8,128)S(1)}, s32[13,256]{1,0:T(8,128)S(1)}) custom-call(f32[64,256]{1,0:T(8,128)} %bitcast.88, s32[13,256]{1,0:T(8,128)} %bitcast.89, s32[1,256]{1,0:T(1,128)} %bitcast.91), custom_call_target="tpu_custom_call" | custom-call | flops 1000000 | bytes 262144 | tf_op jit(solution)/shard_map/pallas_call | solution.py:353
  3.3 2.5 %collective-permute-start.15 = (f32[80,256]{1,0:T(8,128)S(1)}, f32[80,256]{1,0:T(8,128)S(1)}, u32[]{:S(2)}, u32[]{:S(2)}) collective-permute-start(f32[80,256]{1,0:T(8,128)S(1)} %get-tuple-element.59.data_ref), channel_id=1, source_target_pairs={{0,4},{2,6},{4,0},{6,2},{8,12},{10,14},{12,8},{14,10},{16,20},{18,... | collective-permute-start | bytes 245768 | tf_op jit(solution)/shard_map/ppermute | solution.py:30
  5.8 0.0 copy-start
  5.8 1.2 %copy-done = bf16[4,256,512]{2,1,0:T(8,128)(2,1)S(1)} copy-done((bf16[4,256,512]{2,1,0:T(8,128)(2,1)S(1)}, bf16[4,256,512]{2,1,0:T(8,128)(2,1)}, u32[]{:S(2)}) %copy-start) | copy-done | bytes 1048600
  7.1 1.3 %shard_map.49 = (bf16[4,256,512]{2,1,0:T(8,128)(2,1)S(1)}, f32[16,256]{1,0:T(8,128)S(1)}) custom-call(bf16[4,256,512]{2,1,0:T(8,128)(2,1)S(1)} %copy-done, s32[13,256]{1,0:T(8,128)S(1)} %get-tuple-element.60.marks_ref), custom_call_target="tpu_custom_call" | custom-call | flops 1000000 | bytes 262144 | tf_op jit(solution)/shard_map/pallas_call | solution.py:353
  8.3 0.3 collective-permute-done.15.partner_ref
  8.7 13.4 %collective-permute-start.16 = (bf16[2,96,256]{2,1,0:T(8,128)(2,1)S(1)}, bf16[2,96,256]{2,1,0:T(8,128)(2,1)S(1)}, u32[]{:S(2)}, u32[]{:S(2)}) collective-permute-start(bf16[2,96,256]{2,1,0:T(8,128)(2,1)S(1)} %shard_map.51), channel_id=1, source_target_pairs={{0,8},{2,10},{4,12},{6,14},{8,0},{10,2},{12,4},{14,6},{16,24},{18,... | collective-permute-start | bytes 294920 | tf_op jit(solution)/shard_map/ppermute | solution.py:368
  22.1 0.7 %collective-permute-start.17 = (bf16[2,96,256]{2,1,0:T(8,128)(2,1)S(1)}, bf16[2,96,256]{2,1,0:T(8,128)(2,1)S(1)}, u32[]{:S(2)}, u32[]{:S(2)}) collective-permute-start(bf16[2,96,256]{2,1,0:T(8,128)(2,1)S(1)} %shard_map.51), channel_id=1, source_target_pairs={{8,16},{10,18},{12,20},{14,22},{16,8},{18,10},{20,12},{22,14},{9,1... | collective-permute-start | bytes 294920 | tf_op jit(solution)/shard_map/ppermute | solution.py:368
  22.7 0.1 pad_add_fusion.flags_ref
  22.8 2.3 %collective-permute-done.16.three_ref = bf16[2,96,256]{2,1,0:T(8,128)(2,1)S(1)} collective-permute-done((bf16[2,96,256]{2,1,0:T(8,128)(2,1)S(1)}, bf16[2,96,256]{2,1,0:T(8,128)(2,1)S(1)}, u32[]{:S(2)}, u32[]{:S(2)}) %collective-permute-start.16) | collective-permute-done | bytes 98336 | tf_op jit(solution)/shard_map/ppermute | solution.py:368
  25.1 0.0 collective-permute-done.17.four_ref
  25.2 0.6 shard_map.52.same_ref
  25.7 0.1 collective-permute-start.18
  25.8 0.0 collective-permute-done.8.series_ref
  25.8 1.2 %shard_map.50 = f32[16,256]{1,0:T(8,128)S(1)} custom-call(bf16[4,256,512]{2,1,0:T(8,128)(2,1)S(1)} %collective-permute-done.8.series_ref, bf16[4,256,512]{2,1,0:T(8,128)(2,1)S(1)} %get-tuple-element.61.z_ref, s32[13,256]{1,0:T(8,128)S(1)} %get-tuple-element.60.marks_ref, f32[16,256]{1,0:T(8,128)S(1)} %get-tuple-element.62.own_ref), custom_call_target="tpu_custom_call" | custom-call | flops 1000000 | bytes 262144 | tf_op jit(solution)/shard_map/pallas_call | solution.py:353
  27.0 1.6 %collective-permute-start.9 = (f32[16,256]{1,0:T(8,128)S(1)}, f32[16,256]{1,0:T(8,128)S(1)}, u32[]{:S(2)}, u32[]{:S(2)}) collective-permute-start(f32[16,256]{1,0:T(8,128)S(1)} %shard_map.50), channel_id=1, source_target_pairs={{0,1},{1,0},{2,3},{3,2},{4,5},{5,4},{6,7},{7,6},{8,9},{9,8},{10,11... | collective-permute-start | bytes 49160 | tf_op jit(solution)/shard_map/ppermute | solution.py:30
  28.6 2.2 %collective-permute-done.9 = f32[16,256]{1,0:T(8,128)S(1)} collective-permute-done((f32[16,256]{1,0:T(8,128)S(1)}, f32[16,256]{1,0:T(8,128)S(1)}, u32[]{:S(2)}, u32[]{:S(2)}) %collective-permute-start.9) | collective-permute-done | bytes 16416 | tf_op jit(solution)/shard_map/ppermute | solution.py:30
  30.8 0.1 select_convert_fusion
  30.9 0.0 collective-permute-start.10
  30.9 0.1 collective-permute-start.11
  31.0 1.8 %collective-permute-start.12 = (bf16[16,256]{1,0:T(8,128)(2,1)S(1)}, bf16[16,256]{1,0:T(8,128)(2,1)S(1)}, u32[]{:S(2)}, u32[]{:S(2)}) collective-permute-start(bf16[16,256]{1,0:T(8,128)(2,1)S(1)} %get-tuple-element.217), channel_id=1, source_target_pairs={{0,6},{2,4},{4,2},{6,0},{8,14},{10,12},{12,10},{14,8},{16,22},{18,... | collective-permute-start | bytes 24584 | tf_op jit(solution)/shard_map/ppermute | solution.py:30
  32.7 0.0 collective-permute-done.10
  32.7 1.9 %collective-permute-done.11 = bf16[16,256]{1,0:T(8,128)(2,1)S(1)} collective-permute-done((bf16[16,256]{1,0:T(8,128)(2,1)S(1)}, bf16[16,256]{1,0:T(8,128)(2,1)S(1)}, u32[]{:S(2)}, u32[]{:S(2)}) %collective-permute-start.11) | collective-permute-done | bytes 8224 | tf_op jit(solution)/shard_map/ppermute | solution.py:30
  34.6 0.0 collective-permute-done.12
  34.6 4.8 %collective-permute-start.13 = (bf16[4,16,256]{2,1,0:T(8,128)(2,1)S(1)}, bf16[4,16,256]{2,1,0:T(8,128)(2,1)S(1)}, u32[]{:S(2)}, u32[]{:S(2)}) collective-permute-start(bf16[4,16,256]{2,1,0:T(8,128)(2,1)S(1)} %pad_maximum_fusion.refs_0_), channel_id=1, source_target_pairs={{0,8},{2,10},{4,12},{6,14},{8,0},{10,2},{12,4},{14,6},{16,24},{18,... | collective-permute-start | bytes 98312 | tf_op jit(solution)/shard_map/ppermute | solution.py:368
  39.4 0.7 %collective-permute-start.14 = (bf16[4,16,256]{2,1,0:T(8,128)(2,1)S(1)}, bf16[4,16,256]{2,1,0:T(8,128)(2,1)S(1)}, u32[]{:S(2)}, u32[]{:S(2)}) collective-permute-start(bf16[4,16,256]{2,1,0:T(8,128)(2,1)S(1)} %pad_maximum_fusion.refs_0_), channel_id=1, source_target_pairs={{8,16},{10,18},{12,20},{14,22},{16,8},{18,10},{20,12},{22,14},{9,1... | collective-permute-start | bytes 98312 | tf_op jit(solution)/shard_map/ppermute | solution.py:368
  40.1 2.0 %shard_map.53._ = s32[12,256,256]{2,1,0:T(8,128)S(1)} custom-call(s32[2]{0:T(128)S(1)} %pad_add_fusion.flags_ref, f32[6,80,256]{2,1,0:T(8,128)S(1)} %shard_map.52.same_ref), custom_call_target="tpu_custom_call" | custom-call | flops 1000000 | bytes 262144 | tf_op jit(solution)/shard_map/pallas_call | solution.py:353
  42.1 0.0 collective-permute-done.18.other_ref
  42.1 2.1 %shard_map.54 = (s32[12,256,256]{2,1,0:T(8,128)S(1)}, f32[12,64,256]{2,1,0:T(8,128)S(1)}, f32[12,16,256]{2,1,0:T(8,128)S(1)}) custom-call(s32[2]{0:T(128)S(1)} %pad_add_fusion.flags_ref, f32[6,80,256]{2,1,0:T(8,128)S(1)} %shard_map.52.same_ref, f32[6,80,256]{2,1,0:T(8,128)S(1)} %collective-permute-done.18.other_ref, ...), custom_call_target="tpu_custom_call", output_to_operand_aliasing={{0}: (3, {})} | custom-call | flops 1000000 | bytes 262144 | tf_op jit(solution)/shard_map/pallas_call | solution.py:353
  44.2 0.0 copy-start.2
  44.2 0.0 copy-start.3
  44.2 0.0 copy-start.4
  44.2 0.0 collective-permute-done.13.refs_1_
  44.2 0.0 collective-permute-done.14.refs_2_
  44.3 7.3 %shard_map.55 = (f32[64,256]{1,0:T(8,128)S(1)}, f32[32,128]{1,0:T(8,128)S(1)}) custom-call(s32[2]{0:T(128)S(1)} %pad_add_fusion.flags_ref, bf16[4,16,256]{2,1,0:T(8,128)(2,1)S(1)} %pad_maximum_fusion.refs_0_, bf16[4,16,256]{2,1,0:T(8,128)(2,1)S(1)} %collective-permute-done.13.refs_1_, bf16[4,16,256]{2,1,0:T(8,128)(2,1)S(1)} %collective-permute-done.14.refs_2_, ...), custom_call_target="tpu_custom_call" | custom-call | flops 1000000 | bytes 262144 | tf_op jit(solution)/shard_map/pallas_call | solution.py:353
  51.5 3.2 %collective-permute-start.19 = (f32[32,128]{1,0:T(8,128)S(1)}, f32[32,128]{1,0:T(8,128)S(1)}, u32[]{:S(2)}, u32[]{:S(2)}) collective-permute-start(f32[32,128]{1,0:T(8,128)S(1)} %get-tuple-element.66), channel_id=1, source_target_pairs={{0,8},{2,10},{4,12},{6,14},{8,0},{10,2},{12,4},{14,6},{16,24},{18,... | collective-permute-start | bytes 49160 | tf_op jit(solution)/shard_map/ppermute | solution.py:30
  54.7 0.2 collective-permute-start.20
  54.9 2.2 %collective-permute-start.21 = (f32[32,128]{1,0:T(8,128)S(1)}, f32[32,128]{1,0:T(8,128)S(1)}, u32[]{:S(2)}, u32[]{:S(2)}) collective-permute-start(f32[32,128]{1,0:T(8,128)S(1)} %get-tuple-element.66), channel_id=1, source_target_pairs={{0,24},{2,26},{4,28},{6,30},{8,16},{10,18},{12,20},{14,22},{16,8},... | collective-permute-start | bytes 49160 | tf_op jit(solution)/shard_map/ppermute | solution.py:30
  57.1 0.0 collective-permute-done.19
  57.1 2.2 %collective-permute-done.20 = f32[32,128]{1,0:T(8,128)S(1)} collective-permute-done((f32[32,128]{1,0:T(8,128)S(1)}, f32[32,128]{1,0:T(8,128)S(1)}, u32[]{:S(2)}, u32[]{:S(2)}) %collective-permute-start.20) | collective-permute-done | bytes 16416 | tf_op jit(solution)/shard_map/ppermute | solution.py:30
  59.3 1.1 %collective-permute-done.21 = f32[32,128]{1,0:T(8,128)S(1)} collective-permute-done((f32[32,128]{1,0:T(8,128)S(1)}, f32[32,128]{1,0:T(8,128)S(1)}, u32[]{:S(2)}, u32[]{:S(2)}) %collective-permute-start.21) | collective-permute-done | bytes 16416 | tf_op jit(solution)/shard_map/ppermute | solution.py:30
  60.4 2.6 %shard_map.56 = (f32[64,64]{1,0:T(8,128)S(1)}, f32[1,1]{1,0:T(1,128)}) custom-call(f32[32,128]{1,0:T(8,128)S(1)} %add_add_fusion.1.gram_ref), custom_call_target="tpu_custom_call" | custom-call | flops 1000000 | bytes 262144 | tf_op jit(solution)/shard_map/pallas_call | solution.py:353
  63.6 0.0 copy-done.2
  63.7 0.0 copy-done.3
  63.7 0.0 copy-done.4
  63.7 0.4 conditional.1
  63.9 0.2 branch_1_fun.1
  64.1 0.0 copy-start.1
  64.1 0.6 copy-done.1
  (4 shorter events, 0.1 us)
Async XLA Ops:
  0.0 25.8 %collective-permute-start.8 = (bf16[4,256,512]{2,1,0:T(8,128)(2,1)}, bf16[4,256,512]{2,1,0:T(8,128)(2,1)S(1)}, u32[]{:S(2)}, u32[]{:S(2)}) collective-permute-start(bf16[4,256,512]{2,1,0:T(8,128)(2,1)} %series_ref.1), channel_id=1, source_target_pairs={{0,2},{2,4},{4,6},{6,8},{8,10},{10,12},{12,14},{14,16},{16,18},{18... | collective-permute-start | bytes 3145736 | tf_op jit(solution)/shard_map/ppermute | solution.py:51
  3.3 5.3 %collective-permute-start.15 = (f32[80,256]{1,0:T(8,128)S(1)}, f32[80,256]{1,0:T(8,128)S(1)}, u32[]{:S(2)}, u32[]{:S(2)}) collective-permute-start(f32[80,256]{1,0:T(8,128)S(1)} %get-tuple-element.59.data_ref), channel_id=1, source_target_pairs={{0,4},{2,6},{4,0},{6,2},{8,12},{10,14},{12,8},{14,10},{16,20},{18,... | collective-permute-start | bytes 245768 | tf_op jit(solution)/shard_map/ppermute | solution.py:30
  5.8 1.2 %copy-start = (bf16[4,256,512]{2,1,0:T(8,128)(2,1)S(1)}, bf16[4,256,512]{2,1,0:T(8,128)(2,1)}, u32[]{:S(2)}) copy-start(bf16[4,256,512]{2,1,0:T(8,128)(2,1)} %series_ref.1) | copy-start | bytes 3145732
  8.7 16.4 %collective-permute-start.16 = (bf16[2,96,256]{2,1,0:T(8,128)(2,1)S(1)}, bf16[2,96,256]{2,1,0:T(8,128)(2,1)S(1)}, u32[]{:S(2)}, u32[]{:S(2)}) collective-permute-start(bf16[2,96,256]{2,1,0:T(8,128)(2,1)S(1)} %shard_map.51), channel_id=1, source_target_pairs={{0,8},{2,10},{4,12},{6,14},{8,0},{10,2},{12,4},{14,6},{16,24},{18,... | collective-permute-start | bytes 294920 | tf_op jit(solution)/shard_map/ppermute | solution.py:368
  22.1 3.1 %collective-permute-start.17 = (bf16[2,96,256]{2,1,0:T(8,128)(2,1)S(1)}, bf16[2,96,256]{2,1,0:T(8,128)(2,1)S(1)}, u32[]{:S(2)}, u32[]{:S(2)}) collective-permute-start(bf16[2,96,256]{2,1,0:T(8,128)(2,1)S(1)} %shard_map.51), channel_id=1, source_target_pairs={{8,16},{10,18},{12,20},{14,22},{16,8},{18,10},{20,12},{22,14},{9,1... | collective-permute-start | bytes 294920 | tf_op jit(solution)/shard_map/ppermute | solution.py:368
  25.7 16.4 %collective-permute-start.18 = (f32[6,80,256]{2,1,0:T(8,128)S(1)}, f32[6,80,256]{2,1,0:T(8,128)S(1)}, u32[]{:S(2)}, u32[]{:S(2)}) collective-permute-start(f32[6,80,256]{2,1,0:T(8,128)S(1)} %shard_map.52.same_ref), channel_id=1, source_target_pairs={{0,2},{2,0},{4,6},{6,4},{8,10},{10,8},{12,14},{14,12},{16,18},{18,... | collective-permute-start | bytes 1474568 | tf_op jit(solution)/shard_map/ppermute | solution.py:30
  27.0 3.8 %collective-permute-start.9 = (f32[16,256]{1,0:T(8,128)S(1)}, f32[16,256]{1,0:T(8,128)S(1)}, u32[]{:S(2)}, u32[]{:S(2)}) collective-permute-start(f32[16,256]{1,0:T(8,128)S(1)} %shard_map.50), channel_id=1, source_target_pairs={{0,1},{1,0},{2,3},{3,2},{4,5},{5,4},{6,7},{7,6},{8,9},{9,8},{10,11... | collective-permute-start | bytes 49160 | tf_op jit(solution)/shard_map/ppermute | solution.py:30
  30.9 1.9 %collective-permute-start.10 = (bf16[16,256]{1,0:T(8,128)(2,1)S(1)}, bf16[16,256]{1,0:T(8,128)(2,1)S(1)}, u32[]{:S(2)}, u32[]{:S(2)}) collective-permute-start(bf16[16,256]{1,0:T(8,128)(2,1)S(1)} %get-tuple-element.217), channel_id=1, source_target_pairs={{0,2},{2,0},{4,6},{6,4},{8,10},{10,8},{12,14},{14,12},{16,18},{18,... | collective-permute-start | bytes 24584 | tf_op jit(solution)/shard_map/ppermute | solution.py:30
  30.9 3.7 %collective-permute-start.11 = (bf16[16,256]{1,0:T(8,128)(2,1)S(1)}, bf16[16,256]{1,0:T(8,128)(2,1)S(1)}, u32[]{:S(2)}, u32[]{:S(2)}) collective-permute-start(bf16[16,256]{1,0:T(8,128)(2,1)S(1)} %get-tuple-element.217), channel_id=1, source_target_pairs={{0,4},{2,6},{4,0},{6,2},{8,12},{10,14},{12,8},{14,10},{16,20},{18,... | collective-permute-start | bytes 24584 | tf_op jit(solution)/shard_map/ppermute | solution.py:30
  31.0 3.6 %collective-permute-start.12 = (bf16[16,256]{1,0:T(8,128)(2,1)S(1)}, bf16[16,256]{1,0:T(8,128)(2,1)S(1)}, u32[]{:S(2)}, u32[]{:S(2)}) collective-permute-start(bf16[16,256]{1,0:T(8,128)(2,1)S(1)} %get-tuple-element.217), channel_id=1, source_target_pairs={{0,6},{2,4},{4,2},{6,0},{8,14},{10,12},{12,10},{14,8},{16,22},{18,... | collective-permute-start | bytes 24584 | tf_op jit(solution)/shard_map/ppermute | solution.py:30
  34.6 9.6 %collective-permute-start.13 = (bf16[4,16,256]{2,1,0:T(8,128)(2,1)S(1)}, bf16[4,16,256]{2,1,0:T(8,128)(2,1)S(1)}, u32[]{:S(2)}, u32[]{:S(2)}) collective-permute-start(bf16[4,16,256]{2,1,0:T(8,128)(2,1)S(1)} %pad_maximum_fusion.refs_0_), channel_id=1, source_target_pairs={{0,8},{2,10},{4,12},{6,14},{8,0},{10,2},{12,4},{14,6},{16,24},{18,... | collective-permute-start | bytes 98312 | tf_op jit(solution)/shard_map/ppermute | solution.py:368
  39.4 4.8 %collective-permute-start.14 = (bf16[4,16,256]{2,1,0:T(8,128)(2,1)S(1)}, bf16[4,16,256]{2,1,0:T(8,128)(2,1)S(1)}, u32[]{:S(2)}, u32[]{:S(2)}) collective-permute-start(bf16[4,16,256]{2,1,0:T(8,128)(2,1)S(1)} %pad_maximum_fusion.refs_0_), channel_id=1, source_target_pairs={{8,16},{10,18},{12,20},{14,22},{16,8},{18,10},{20,12},{22,14},{9,1... | collective-permute-start | bytes 98312 | tf_op jit(solution)/shard_map/ppermute | solution.py:368
  44.2 19.4 %copy-start.2 = (f32[256,64]{0,1:T(8,128)S(1)}, f32[256,64]{0,1:T(8,128)}, u32[]{:S(2)}) copy-start(f32[256,64]{0,1:T(8,128)} %param.11) | copy-start | bytes 196612
  44.2 19.4 %copy-start.3 = (s32[256,13]{0,1:T(8,128)S(1)}, s32[256,13]{0,1:T(8,128)}, u32[]{:S(2)}) copy-start(s32[256,13]{0,1:T(8,128)} %param.10) | copy-start | bytes 39940
  44.2 19.4 %copy-start.4 = (s32[256]{0:T(256)S(1)}, s32[256]{0:T(256)}, u32[]{:S(2)}) copy-start(s32[256]{0:T(256)} %param.9) | copy-start | bytes 3076
  51.5 5.6 %collective-permute-start.19 = (f32[32,128]{1,0:T(8,128)S(1)}, f32[32,128]{1,0:T(8,128)S(1)}, u32[]{:S(2)}, u32[]{:S(2)}) collective-permute-start(f32[32,128]{1,0:T(8,128)S(1)} %get-tuple-element.66), channel_id=1, source_target_pairs={{0,8},{2,10},{4,12},{6,14},{8,0},{10,2},{12,4},{14,6},{16,24},{18,... | collective-permute-start | bytes 49160 | tf_op jit(solution)/shard_map/ppermute | solution.py:30
  54.7 4.6 %collective-permute-start.20 = (f32[32,128]{1,0:T(8,128)S(1)}, f32[32,128]{1,0:T(8,128)S(1)}, u32[]{:S(2)}, u32[]{:S(2)}) collective-permute-start(f32[32,128]{1,0:T(8,128)S(1)} %get-tuple-element.66), channel_id=1, source_target_pairs={{0,16},{2,18},{4,20},{6,22},{8,24},{10,26},{12,28},{14,30},{16,0},... | collective-permute-start | bytes 49160 | tf_op jit(solution)/shard_map/ppermute | solution.py:30
  54.9 5.5 %collective-permute-start.21 = (f32[32,128]{1,0:T(8,128)S(1)}, f32[32,128]{1,0:T(8,128)S(1)}, u32[]{:S(2)}, u32[]{:S(2)}) collective-permute-start(f32[32,128]{1,0:T(8,128)S(1)} %get-tuple-element.66), channel_id=1, source_target_pairs={{0,24},{2,26},{4,28},{6,30},{8,16},{10,18},{12,20},{14,22},{16,8},... | collective-permute-start | bytes 49160 | tf_op jit(solution)/shard_map/ppermute | solution.py:30
  64.1 0.6 copy-start.1
where the time goes:
time: 65 us; the launch traced here: 64.7 us
  starting transfers between devices  33.5 us (52%)
  Pallas kernels  18 us (28%)
  waiting for transfers between devices  10 us (15%)
  local copies, waits for them, and re-layouts  1.87 us (3%)
  between operations  0.87 us (1%)
    ppermute x4, starting transfers between devices, pairwise(): lax.ppermute(value, 'vox', [(i, j) for i, j in pairs if 0 <= j < count])  19.5 us
    pallas_call x10, Pallas kernels, call(): pl.pallas_call(kernel, out_shape=outs, in_specs=[first] + [VMEM] * (len(a...  18 us
    ppermute x9, starting transfers between devices, exchanged(): return lax.ppermute(value, axis, [(i, i ^ distance) for i in range(count)])  11.6 us
    ppermute x9, waiting for transfers between devices, exchanged(): return lax.ppermute(value, axis, [(i, i ^ distance) for i in range(count)])  7.7 us
    ppermute x1, starting transfers between devices, shifted(): return lax.ppermute(shard, axis, pairs)  2.45 us
    ppermute x4, waiting for transfers between devices, pairwise(): lax.ppermute(value, 'vox', [(i, j) for i, j in pairs if 0 <= j < count])  2.34 us
    unnamed x10, local copies, waits for them, and re-layouts  1.87 us
  transfers between devices with their start and end apart: 14, of which 6 were waited for; matrix products, arithmetic and copies ran while one was open for 0% of the time, Pallas kernels for 12%

commit v1 on v0

--- a/solution.py
+++ b/solution.py
@@ -36,7 +36,10 @@
         return lax.psum(value, axis) / stride
     while stride < count:
         if stride > 1 and 4 * stride <= count:
-            first, second, third = (exchanged(value, axis, k * stride) for k in (1, 2, 3))
+            parts = []
+            for k in (1, 2, 3):
+                parts.append(exchanged(value, axis, k * stride))
+            first, second, third = parts
             value = (value + first) + (second + third)
             stride *= 4
         else:
@@ -232,7 +235,7 @@
         scale_ref[b] = jnp.broadcast_to(live * lax.rsqrt(degree), scale_ref.shape[1:])
         return carry
 
-    lax.fori_loop(1, count - 1, dense, 0)
+    lax.fori_loop(1, count - 1, dense, 0, unroll=2)
 
     scales = {b: scale_ref[b, 0:1, :] for b in range(1, count - 1)}
     vectors = {b: vec_ref[b] for b in range(1, count - 1)}

time: 65 us -> 64.6 us (level)
  no operation moved by 1% of the time
where the time goes in v1:
time: 64.6 us; the launch traced here: 64.4 us
  starting transfers between devices  33.5 us (52%)
  Pallas kernels  17.6 us (27%)
  waiting for transfers between devices  10 us (15%)
  local copies, waits for them, and re-layouts  1.87 us (3%)
  between operations  0.87 us (1%)
    ppermute x4, starting transfers between devices, pairwise(): lax.ppermute(value, 'vox', [(i, j) for i, j in pairs if 0 <= j < count])  19.5 us
    pallas_call x10, Pallas kernels, call(): pl.pallas_call(kernel, out_shape=outs, in_specs=[first] + [VMEM] * (len(a...  17.6 us
    ppermute x9, starting transfers between devices, exchanged(): return lax.ppermute(value, axis, [(i, i ^ distance) for i in range(count)])  11.6 us
    ppermute x9, waiting for transfers between devices, exchanged(): return lax.ppermute(value, axis, [(i, i ^ distance) for i in range(count)])  7.7 us
    ppermute x1, starting transfers between devices, shifted(): return lax.ppermute(shard, axis, pairs)  2.45 us
    ppermute x4, waiting for transfers between devices, pairwise(): lax.ppermute(value, 'vox', [(i, j) for i, j in pairs if 0 <= j < count])  2.34 us
    unnamed x10, local copies, waits for them, and re-layouts  1.87 us
  transfers between devices with their start and end apart: 14, of which 6 were waited for; matrix products, arithmetic and copies ran while one was open for 0% of the time, Pallas kernels for 12%

profile of v1, /device:TPU:0, one launch (start us, length us, event | category | flops | bytes accessed | tf_op | source)
XLA Modules:
  0.0 64.4 jit_solution(2973643911180103841)
XLA Ops:
  0.0 2.5 %collective-permute-start.8 = (bf16[4,256,512]{2,1,0:T(8,128)(2,1)}, bf16[4,256,512]{2,1,0:T(8,128)(2,1)S(1)}, u32[]{:S(2)}, u32[]{:S(2)}) collective-permute-start(bf16[4,256,512]{2,1,0:T(8,128)(2,1)} %series_ref.1), channel_id=1, source_target_pairs={{0,2},{2,4},{4,6},{6,8},{8,10},{10,12},{12,14},{14,16},{16,18},{18... | collective-permute-start | bytes 3145736 | tf_op jit(solution)/shard_map/ppermute | solution.py:54
  2.5 0.9 %shard_map.48 = (f32[80,256]{1,0:T(8,128)S(1)}, s32[13,256]{1,0:T(8,128)S(1)}) custom-call(f32[64,256]{1,0:T(8,128)} %bitcast.88, s32[13,256]{1,0:T(8,128)} %bitcast.89, s32[1,256]{1,0:T(1,128)} %bitcast.91), custom_call_target="tpu_custom_call" | custom-call | flops 1000000 | bytes 262144 | tf_op jit(solution)/shard_map/pallas_call | solution.py:356
  3.3 2.5 %collective-permute-start.15 = (f32[80,256]{1,0:T(8,128)S(1)}, f32[80,256]{1,0:T(8,128)S(1)}, u32[]{:S(2)}, u32[]{:S(2)}) collective-permute-start(f32[80,256]{1,0:T(8,128)S(1)} %get-tuple-element.59.data_ref), channel_id=1, source_target_pairs={{0,4},{2,6},{4,0},{6,2},{8,12},{10,14},{12,8},{14,10},{16,20},{18,... | collective-permute-start | bytes 245768 | tf_op jit(solution)/shard_map/ppermute | solution.py:30
  5.8 0.0 copy-start
  5.8 1.2 %copy-done = bf16[4,256,512]{2,1,0:T(8,128)(2,1)S(1)} copy-done((bf16[4,256,512]{2,1,0:T(8,128)(2,1)S(1)}, bf16[4,256,512]{2,1,0:T(8,128)(2,1)}, u32[]{:S(2)}) %copy-start) | copy-done | bytes 1048600
  7.1 1.3 %shard_map.49 = (bf16[4,256,512]{2,1,0:T(8,128)(2,1)S(1)}, f32[16,256]{1,0:T(8,128)S(1)}) custom-call(bf16[4,256,512]{2,1,0:T(8,128)(2,1)S(1)} %copy-done, s32[13,256]{1,0:T(8,128)S(1)} %get-tuple-element.60.marks_ref), custom_call_target="tpu_custom_call" | custom-call | flops 1000000 | bytes 262144 | tf_op jit(solution)/shard_map/pallas_call | solution.py:356
  8.3 0.3 collective-permute-done.15.partner_ref
  8.7 13.4 %collective-permute-start.16 = (bf16[2,96,256]{2,1,0:T(8,128)(2,1)S(1)}, bf16[2,96,256]{2,1,0:T(8,128)(2,1)S(1)}, u32[]{:S(2)}, u32[]{:S(2)}) collective-permute-start(bf16[2,96,256]{2,1,0:T(8,128)(2,1)S(1)} %shard_map.51), channel_id=1, source_target_pairs={{0,8},{2,10},{4,12},{6,14},{8,0},{10,2},{12,4},{14,6},{16,24},{18,... | collective-permute-start | bytes 294920 | tf_op jit(solution)/shard_map/ppermute | solution.py:371
  22.1 0.7 %collective-permute-start.17 = (bf16[2,96,256]{2,1,0:T(8,128)(2,1)S(1)}, bf16[2,96,256]{2,1,0:T(8,128)(2,1)S(1)}, u32[]{:S(2)}, u32[]{:S(2)}) collective-permute-start(bf16[2,96,256]{2,1,0:T(8,128)(2,1)S(1)} %shard_map.51), channel_id=1, source_target_pairs={{8,16},{10,18},{12,20},{14,22},{16,8},{18,10},{20,12},{22,14},{9,1... | collective-permute-start | bytes 294920 | tf_op jit(solution)/shard_map/ppermute | solution.py:371
  22.7 0.1 pad_add_fusion.flags_ref
  22.8 2.3 %collective-permute-done.16.three_ref = bf16[2,96,256]{2,1,0:T(8,128)(2,1)S(1)} collective-permute-done((bf16[2,96,256]{2,1,0:T(8,128)(2,1)S(1)}, bf16[2,96,256]{2,1,0:T(8,128)(2,1)S(1)}, u32[]{:S(2)}, u32[]{:S(2)}) %collective-permute-start.16) | collective-permute-done | bytes 98336 | tf_op jit(solution)/shard_map/ppermute | solution.py:371
  25.1 0.0 collective-permute-done.17.four_ref
  25.2 0.6 shard_map.52.same_ref
  25.7 0.1 collective-permute-start.18
  25.8 0.0 collective-permute-done.8.series_ref
  25.8 1.2 %shard_map.50 = f32[16,256]{1,0:T(8,128)S(1)} custom-call(bf16[4,256,512]{2,1,0:T(8,128)(2,1)S(1)} %collective-permute-done.8.series_ref, bf16[4,256,512]{2,1,0:T(8,128)(2,1)S(1)} %get-tuple-element.61.z_ref, s32[13,256]{1,0:T(8,128)S(1)} %get-tuple-element.60.marks_ref, f32[16,256]{1,0:T(8,128)S(1)} %get-tuple-element.62.own_ref), custom_call_target="tpu_custom_call" | custom-call | flops 1000000 | bytes 262144 | tf_op jit(solution)/shard_map/pallas_call | solution.py:356
  27.0 1.6 %collective-permute-start.9 = (f32[16,256]{1,0:T(8,128)S(1)}, f32[16,256]{1,0:T(8,128)S(1)}, u32[]{:S(2)}, u32[]{:S(2)}) collective-permute-start(f32[16,256]{1,0:T(8,128)S(1)} %shard_map.50), channel_id=1, source_target_pairs={{0,1},{1,0},{2,3},{3,2},{4,5},{5,4},{6,7},{7,6},{8,9},{9,8},{10,11... | collective-permute-start | bytes 49160 | tf_op jit(solution)/shard_map/ppermute | solution.py:30
  28.6 2.2 %collective-permute-done.9 = f32[16,256]{1,0:T(8,128)S(1)} collective-permute-done((f32[16,256]{1,0:T(8,128)S(1)}, f32[16,256]{1,0:T(8,128)S(1)}, u32[]{:S(2)}, u32[]{:S(2)}) %collective-permute-start.9) | collective-permute-done | bytes 16416 | tf_op jit(solution)/shard_map/ppermute | solution.py:30
  30.8 0.1 select_convert_fusion
  30.9 0.0 collective-permute-start.10
  30.9 0.1 collective-permute-start.11
  31.0 1.8 %collective-permute-start.12 = (bf16[16,256]{1,0:T(8,128)(2,1)S(1)}, bf16[16,256]{1,0:T(8,128)(2,1)S(1)}, u32[]{:S(2)}, u32[]{:S(2)}) collective-permute-start(bf16[16,256]{1,0:T(8,128)(2,1)S(1)} %get-tuple-element.217), channel_id=1, source_target_pairs={{0,6},{2,4},{4,2},{6,0},{8,14},{10,12},{12,10},{14,8},{16,22},{18,... | collective-permute-start | bytes 24584 | tf_op jit(solution)/shard_map/ppermute | solution.py:30
  32.7 0.0 collective-permute-done.10
  32.7 1.9 %collective-permute-done.11 = bf16[16,256]{1,0:T(8,128)(2,1)S(1)} collective-permute-done((bf16[16,256]{1,0:T(8,128)(2,1)S(1)}, bf16[16,256]{1,0:T(8,128)(2,1)S(1)}, u32[]{:S(2)}, u32[]{:S(2)}) %collective-permute-start.11) | collective-permute-done | bytes 8224 | tf_op jit(solution)/shard_map/ppermute | solution.py:30
  34.6 0.0 collective-permute-done.12
  34.6 4.8 %collective-permute-start.13 = (bf16[4,16,256]{2,1,0:T(8,128)(2,1)S(1)}, bf16[4,16,256]{2,1,0:T(8,128)(2,1)S(1)}, u32[]{:S(2)}, u32[]{:S(2)}) collective-permute-start(bf16[4,16,256]{2,1,0:T(8,128)(2,1)S(1)} %pad_maximum_fusion.refs_0_), channel_id=1, source_target_pairs={{0,8},{2,10},{4,12},{6,14},{8,0},{10,2},{12,4},{14,6},{16,24},{18,... | collective-permute-start | bytes 98312 | tf_op jit(solution)/shard_map/ppermute | solution.py:371
  39.4 0.7 %collective-permute-start.14 = (bf16[4,16,256]{2,1,0:T(8,128)(2,1)S(1)}, bf16[4,16,256]{2,1,0:T(8,128)(2,1)S(1)}, u32[]{:S(2)}, u32[]{:S(2)}) collective-permute-start(bf16[4,16,256]{2,1,0:T(8,128)(2,1)S(1)} %pad_maximum_fusion.refs_0_), channel_id=1, source_target_pairs={{8,16},{10,18},{12,20},{14,22},{16,8},{18,10},{20,12},{22,14},{9,1... | collective-permute-start | bytes 98312 | tf_op jit(solution)/shard_map/ppermute | solution.py:371
  40.1 2.0 %shard_map.53._ = s32[12,256,256]{2,1,0:T(8,128)S(1)} custom-call(s32[2]{0:T(128)S(1)} %pad_add_fusion.flags_ref, f32[6,80,256]{2,1,0:T(8,128)S(1)} %shard_map.52.same_ref), custom_call_target="tpu_custom_call" | custom-call | flops 1000000 | bytes 262144 | tf_op jit(solution)/shard_map/pallas_call | solution.py:356
  42.1 0.0 collective-permute-done.18.other_ref
  42.1 2.1 %shard_map.54 = (s32[12,256,256]{2,1,0:T(8,128)S(1)}, f32[12,64,256]{2,1,0:T(8,128)S(1)}, f32[12,16,256]{2,1,0:T(8,128)S(1)}) custom-call(s32[2]{0:T(128)S(1)} %pad_add_fusion.flags_ref, f32[6,80,256]{2,1,0:T(8,128)S(1)} %shard_map.52.same_ref, f32[6,80,256]{2,1,0:T(8,128)S(1)} %collective-permute-done.18.other_ref, ...), custom_call_target="tpu_custom_call", output_to_operand_aliasing={{0}: (3, {})} | custom-call | flops 1000000 | bytes 262144 | tf_op jit(solution)/shard_map/pallas_call | solution.py:356
  44.2 0.0 copy-start.2
  44.2 0.0 copy-start.3
  44.2 0.0 copy-start.4
  44.2 0.0 collective-permute-done.13.refs_1_
  44.2 0.0 collective-permute-done.14.refs_2_
  44.3 6.9 %shard_map.55 = (f32[64,256]{1,0:T(8,128)S(1)}, f32[32,128]{1,0:T(8,128)S(1)}) custom-call(s32[2]{0:T(128)S(1)} %pad_add_fusion.flags_ref, bf16[4,16,256]{2,1,0:T(8,128)(2,1)S(1)} %pad_maximum_fusion.refs_0_, bf16[4,16,256]{2,1,0:T(8,128)(2,1)S(1)} %collective-permute-done.13.refs_1_, bf16[4,16,256]{2,1,0:T(8,128)(2,1)S(1)} %collective-permute-done.14.refs_2_, ...), custom_call_target="tpu_custom_call" | custom-call | flops 1000000 | bytes 262144 | tf_op jit(solution)/shard_map/pallas_call | solution.py:356
  51.2 3.2 %collective-permute-start.19 = (f32[32,128]{1,0:T(8,128)S(1)}, f32[32,128]{1,0:T(8,128)S(1)}, u32[]{:S(2)}, u32[]{:S(2)}) collective-permute-start(f32[32,128]{1,0:T(8,128)S(1)} %get-tuple-element.66), channel_id=1, source_target_pairs={{0,8},{2,10},{4,12},{6,14},{8,0},{10,2},{12,4},{14,6},{16,24},{18,... | collective-permute-start | bytes 49160 | tf_op jit(solution)/shard_map/ppermute | solution.py:30
  54.3 0.2 collective-permute-start.20
  54.5 2.2 %collective-permute-start.21 = (f32[32,128]{1,0:T(8,128)S(1)}, f32[32,128]{1,0:T(8,128)S(1)}, u32[]{:S(2)}, u32[]{:S(2)}) collective-permute-start(f32[32,128]{1,0:T(8,128)S(1)} %get-tuple-element.66), channel_id=1, source_target_pairs={{0,24},{2,26},{4,28},{6,30},{8,16},{10,18},{12,20},{14,22},{16,8},... | collective-permute-start | bytes 49160 | tf_op jit(solution)/shard_map/ppermute | solution.py:30
  56.8 0.0 collective-permute-done.19
  56.8 2.2 %collective-permute-done.20 = f32[32,128]{1,0:T(8,128)S(1)} collective-permute-done((f32[32,128]{1,0:T(8,128)S(1)}, f32[32,128]{1,0:T(8,128)S(1)}, u32[]{:S(2)}, u32[]{:S(2)}) %collective-permute-start.20) | collective-permute-done | bytes 16416 | tf_op jit(solution)/shard_map/ppermute | solution.py:30
  59.0 1.1 %collective-permute-done.21 = f32[32,128]{1,0:T(8,128)S(1)} collective-permute-done((f32[32,128]{1,0:T(8,128)S(1)}, f32[32,128]{1,0:T(8,128)S(1)}, u32[]{:S(2)}, u32[]{:S(2)}) %collective-permute-start.21) | collective-permute-done | bytes 16416 | tf_op jit(solution)/shard_map/ppermute | solution.py:30
  60.1 2.6 %shard_map.56 = (f32[64,64]{1,0:T(8,128)S(1)}, f32[1,1]{1,0:T(1,128)}) custom-call(f32[32,128]{1,0:T(8,128)S(1)} %add_add_fusion.1.gram_ref), custom_call_target="tpu_custom_call" | custom-call | flops 1000000 | bytes 262144 | tf_op jit(solution)/shard_map/pallas_call | solution.py:356
  63.3 0.0 copy-done.2
  63.3 0.0 copy-done.3
  63.3 0.0 copy-done.4
  63.3 0.4 conditional.1
  63.5 0.2 branch_1_fun.1
  63.7 0.0 copy-start.1
  63.8 0.6 copy-done.1
  (4 shorter events, 0.1 us)
Async XLA Ops:
  0.0 25.8 %collective-permute-start.8 = (bf16[4,256,512]{2,1,0:T(8,128)(2,1)}, bf16[4,256,512]{2,1,0:T(8,128)(2,1)S(1)}, u32[]{:S(2)}, u32[]{:S(2)}) collective-permute-start(bf16[4,256,512]{2,1,0:T(8,128)(2,1)} %series_ref.1), channel_id=1, source_target_pairs={{0,2},{2,4},{4,6},{6,8},{8,10},{10,12},{12,14},{14,16},{16,18},{18... | collective-permute-start | bytes 3145736 | tf_op jit(solution)/shard_map/ppermute | solution.py:54
  3.3 5.3 %collective-permute-start.15 = (f32[80,256]{1,0:T(8,128)S(1)}, f32[80,256]{1,0:T(8,128)S(1)}, u32[]{:S(2)}, u32[]{:S(2)}) collective-permute-start(f32[80,256]{1,0:T(8,128)S(1)} %get-tuple-element.59.data_ref), channel_id=1, source_target_pairs={{0,4},{2,6},{4,0},{6,2},{8,12},{10,14},{12,8},{14,10},{16,20},{18,... | collective-permute-start | bytes 245768 | tf_op jit(solution)/shard_map/ppermute | solution.py:30
  5.8 1.2 %copy-start = (bf16[4,256,512]{2,1,0:T(8,128)(2,1)S(1)}, bf16[4,256,512]{2,1,0:T(8,128)(2,1)}, u32[]{:S(2)}) copy-start(bf16[4,256,512]{2,1,0:T(8,128)(2,1)} %series_ref.1) | copy-start | bytes 3145732
  8.7 16.4 %collective-permute-start.16 = (bf16[2,96,256]{2,1,0:T(8,128)(2,1)S(1)}, bf16[2,96,256]{2,1,0:T(8,128)(2,1)S(1)}, u32[]{:S(2)}, u32[]{:S(2)}) collective-permute-start(bf16[2,96,256]{2,1,0:T(8,128)(2,1)S(1)} %shard_map.51), channel_id=1, source_target_pairs={{0,8},{2,10},{4,12},{6,14},{8,0},{10,2},{12,4},{14,6},{16,24},{18,... | collective-permute-start | bytes 294920 | tf_op jit(solution)/shard_map/ppermute | solution.py:371
  22.1 3.1 %collective-permute-start.17 = (bf16[2,96,256]{2,1,0:T(8,128)(2,1)S(1)}, bf16[2,96,256]{2,1,0:T(8,128)(2,1)S(1)}, u32[]{:S(2)}, u32[]{:S(2)}) collective-permute-start(bf16[2,96,256]{2,1,0:T(8,128)(2,1)S(1)} %shard_map.51), channel_id=1, source_target_pairs={{8,16},{10,18},{12,20},{14,22},{16,8},{18,10},{20,12},{22,14},{9,1... | collective-permute-start | bytes 294920 | tf_op jit(solution)/shard_map/ppermute | solution.py:371
  25.7 16.4 %collective-permute-start.18 = (f32[6,80,256]{2,1,0:T(8,128)S(1)}, f32[6,80,256]{2,1,0:T(8,128)S(1)}, u32[]{:S(2)}, u32[]{:S(2)}) collective-permute-start(f32[6,80,256]{2,1,0:T(8,128)S(1)} %shard_map.52.same_ref), channel_id=1, source_target_pairs={{0,2},{2,0},{4,6},{6,4},{8,10},{10,8},{12,14},{14,12},{16,18},{18,... | collective-permute-start | bytes 1474568 | tf_op jit(solution)/shard_map/ppermute | solution.py:30
  27.0 3.8 %collective-permute-start.9 = (f32[16,256]{1,0:T(8,128)S(1)}, f32[16,256]{1,0:T(8,128)S(1)}, u32[]{:S(2)}, u32[]{:S(2)}) collective-permute-start(f32[16,256]{1,0:T(8,128)S(1)} %shard_map.50), channel_id=1, source_target_pairs={{0,1},{1,0},{2,3},{3,2},{4,5},{5,4},{6,7},{7,6},{8,9},{9,8},{10,11... | collective-permute-start | bytes 49160 | tf_op jit(solution)/shard_map/ppermute | solution.py:30
  30.9 1.9 %collective-permute-start.10 = (bf16[16,256]{1,0:T(8,128)(2,1)S(1)}, bf16[16,256]{1,0:T(8,128)(2,1)S(1)}, u32[]{:S(2)}, u32[]{:S(2)}) collective-permute-start(bf16[16,256]{1,0:T(8,128)(2,1)S(1)} %get-tuple-element.217), channel_id=1, source_target_pairs={{0,2},{2,0},{4,6},{6,4},{8,10},{10,8},{12,14},{14,12},{16,18},{18,... | collective-permute-start | bytes 24584 | tf_op jit(solution)/shard_map/ppermute | solution.py:30
  30.9 3.7 %collective-permute-start.11 = (bf16[16,256]{1,0:T(8,128)(2,1)S(1)}, bf16[16,256]{1,0:T(8,128)(2,1)S(1)}, u32[]{:S(2)}, u32[]{:S(2)}) collective-permute-start(bf16[16,256]{1,0:T(8,128)(2,1)S(1)} %get-tuple-element.217), channel_id=1, source_target_pairs={{0,4},{2,6},{4,0},{6,2},{8,12},{10,14},{12,8},{14,10},{16,20},{18,... | collective-permute-start | bytes 24584 | tf_op jit(solution)/shard_map/ppermute | solution.py:30
  31.0 3.6 %collective-permute-start.12 = (bf16[16,256]{1,0:T(8,128)(2,1)S(1)}, bf16[16,256]{1,0:T(8,128)(2,1)S(1)}, u32[]{:S(2)}, u32[]{:S(2)}) collective-permute-start(bf16[16,256]{1,0:T(8,128)(2,1)S(1)} %get-tuple-element.217), channel_id=1, source_target_pairs={{0,6},{2,4},{4,2},{6,0},{8,14},{10,12},{12,10},{14,8},{16,22},{18,... | collective-permute-start | bytes 24584 | tf_op jit(solution)/shard_map/ppermute | solution.py:30
  34.6 9.6 %collective-permute-start.13 = (bf16[4,16,256]{2,1,0:T(8,128)(2,1)S(1)}, bf16[4,16,256]{2,1,0:T(8,128)(2,1)S(1)}, u32[]{:S(2)}, u32[]{:S(2)}) collective-permute-start(bf16[4,16,256]{2,1,0:T(8,128)(2,1)S(1)} %pad_maximum_fusion.refs_0_), channel_id=1, source_target_pairs={{0,8},{2,10},{4,12},{6,14},{8,0},{10,2},{12,4},{14,6},{16,24},{18,... | collective-permute-start | bytes 98312 | tf_op jit(solution)/shard_map/ppermute | solution.py:371
  39.4 4.8 %collective-permute-start.14 = (bf16[4,16,256]{2,1,0:T(8,128)(2,1)S(1)}, bf16[4,16,256]{2,1,0:T(8,128)(2,1)S(1)}, u32[]{:S(2)}, u32[]{:S(2)}) collective-permute-start(bf16[4,16,256]{2,1,0:T(8,128)(2,1)S(1)} %pad_maximum_fusion.refs_0_), channel_id=1, source_target_pairs={{8,16},{10,18},{12,20},{14,22},{16,8},{18,10},{20,12},{22,14},{9,1... | collective-permute-start | bytes 98312 | tf_op jit(solution)/shard_map/ppermute | solution.py:371
  44.2 19.1 %copy-start.2 = (f32[256,64]{0,1:T(8,128)S(1)}, f32[256,64]{0,1:T(8,128)}, u32[]{:S(2)}) copy-start(f32[256,64]{0,1:T(8,128)} %param.11) | copy-start | bytes 196612
  44.2 19.1 %copy-start.3 = (s32[256,13]{0,1:T(8,128)S(1)}, s32[256,13]{0,1:T(8,128)}, u32[]{:S(2)}) copy-start(s32[256,13]{0,1:T(8,128)} %param.10) | copy-start | bytes 39940
  44.2 19.1 %copy-start.4 = (s32[256]{0:T(256)S(1)}, s32[256]{0:T(256)}, u32[]{:S(2)}) copy-start(s32[256]{0:T(256)} %param.9) | copy-start | bytes 3076
  51.2 5.6 %collective-permute-start.19 = (f32[32,128]{1,0:T(8,128)S(1)}, f32[32,128]{1,0:T(8,128)S(1)}, u32[]{:S(2)}, u32[]{:S(2)}) collective-permute-start(f32[32,128]{1,0:T(8,128)S(1)} %get-tuple-element.66), channel_id=1, source_target_pairs={{0,8},{2,10},{4,12},{6,14},{8,0},{10,2},{12,4},{14,6},{16,24},{18,... | collective-permute-start | bytes 49160 | tf_op jit(solution)/shard_map/ppermute | solution.py:30
  54.3 4.6 %collective-permute-start.20 = (f32[32,128]{1,0:T(8,128)S(1)}, f32[32,128]{1,0:T(8,128)S(1)}, u32[]{:S(2)}, u32[]{:S(2)}) collective-permute-start(f32[32,128]{1,0:T(8,128)S(1)} %get-tuple-element.66), channel_id=1, source_target_pairs={{0,16},{2,18},{4,20},{6,22},{8,24},{10,26},{12,28},{14,30},{16,0},... | collective-permute-start | bytes 49160 | tf_op jit(solution)/shard_map/ppermute | solution.py:30
  54.5 5.5 %collective-permute-start.21 = (f32[32,128]{1,0:T(8,128)S(1)}, f32[32,128]{1,0:T(8,128)S(1)}, u32[]{:S(2)}, u32[]{:S(2)}) collective-permute-start(f32[32,128]{1,0:T(8,128)S(1)} %get-tuple-element.66), channel_id=1, source_target_pairs={{0,24},{2,26},{4,28},{6,30},{8,16},{10,18},{12,20},{14,22},{16,8},... | collective-permute-start | bytes 49160 | tf_op jit(solution)/shard_map/ppermute | solution.py:30
  63.7 0.6 copy-start.1
